TPU v7x, 32 devices: a whole 2x2x4 slice. The times are simulated.
32 devices in a mesh: gx: 8 (over z, core), gy: 4 (over y, x).
Axes of the slice: x: 2, y: 2, z: 4, core: 2. Of those that a mesh axis runs over, the one named last changes fastest.
Arguments:
- velocity: float32 [3, 128, 64, 128], P(None, 'gx', 'gy'), may hold values from -6 to 6
- stresses: float32 [6, 128, 64, 128], P(None, 'gx', 'gy'), may hold values from -6 to 6
- buoyancy: float32 [128, 64, 128], P('gx', 'gy'), may hold values from 0.3 to 0.6
- lame_first: float32 [128, 64, 128], P('gx', 'gy'), may hold values from 0.05 to 0.15
- rigidity: float32 [128, 64, 128], P('gx', 'gy'), may hold values from 0.04 to 0.12
- histories: bfloat16 [8192, 512], P(('gx', 'gy')), may hold values from -6 to 6
- mechanism: bfloat16 [8192, 6], P(('gx', 'gy')), may hold values from -6 to 6
- resample: bfloat16 [512, 3], replicated, may hold values from -0.25 to 0.25
- owners: int32 [8192, 1], P(('gx', 'gy')), may hold values from 0 to 3; in each aligned block of 256 rows (0 to 255, 256 to 511, ...) at most 64 rows name the same one
- cell_offsets: int32 [8192], P(('gx', 'gy')), may hold values from 0 to 32767
Outputs:
- velocity_out: float32 [3, 128, 64, 128], P(None, 'gx', 'gy')
- stresses_out: float32 [6, 128, 64, 128], P(None, 'gx', 'gy')
Inputs may be any that keep to these rules, and one draw needn't show every extreme that they name: `owners`: among the 256 rows of one device at most 64 name the same owner, a bound that some block reaches of them. `cell_offsets`: cell index x * 16 * 128 + y * 128 + z within the enclosing block.
All inputs are finite; a program needn't handle non-finite values.
Results may differ from a plain program's by a relative error of at most 0.00052.
Values may be sent and summed in bfloat16 or wider, within the bound.
A program may use at most 64 MiB of HBM per device.

v0:
```python
import functools

import jax
import jax.numpy as jnp
from jax import lax
from jax.experimental import pallas as pl
from jax.experimental.pallas import tpu as pltpu
from jax.sharding import PartitionSpec as P

A = 9.0 / 8.0
B = -1.0 / 24.0
MESH = pl.DeviceIdType.MESH
XP = 2
YP = 8

STRESS_FACES = (((0, True), (3, False), (4, False)), ((3, False), (1, True), (5, False)))
VELOCITY_FACES = (((0, False), (1, True), (2, True)), ((0, True), (1, False), (2, True)))


def face_layers(faces, up, extent):
    out = []
    for comp, forward in faces:
        if up:
            out += [(comp, extent - 1, not forward)]
            out += [] if forward else [(comp, extent - 2, False)]
        else:
            out += [(comp, 0, forward)]
            out += [(comp, 1, False)] if forward else []
    return out


def face_slots(faces, up, extent):
    return sum(2 if wide else 1 for _, _, wide in face_layers(faces, up, extent))


def halo_terms(faces, from_low, extent, halo):
    out, at = [], 0
    for comp, forward in faces:
        if from_low == forward:
            sign = -B if from_low else B
            out.append((comp, 0 if from_low else extent - 1, sign * halo(at)))
            at += 1
            continue
        first, second = halo(at) + halo(at + 1), halo(at + 2)
        at += 3
        if from_low:
            out.append((comp, 0, -A * first - B * second))
            out.append((comp, 1, -B * first))
        else:
            out.append((comp, extent - 1, A * first + B * second))
            out.append((comp, extent - 2, B * first))
    return out


def kernel(
    groups, blocks, steps,
    v_hbm, s_hbm, buoy_hbm, lame_hbm, rig_hbm, hist_hbm, mech_hbm, res_hbm, own_hbm, off_hbm,
    v_out, s_out,
    V, S, buoy, lame, rig, hist, mech_ref, res_ref, own_ref, off_ref, src, gathered, plane_hot, level_hot,
    send_x, recv_x, send_y, recv_y,
    stress_sem, load_sem, src_send, src_recv, face_send, face_recv,
):
    gx = lax.axis_index("gx")
    gy = lax.axis_index("gy")
    cx, cy, cz = buoy.shape
    rows = hist.shape[0]
    inner = (slice(None), pl.ds(XP, cx), pl.ds(YP, cy), slice(None))

    barrier = pltpu.get_barrier_semaphore()
    sides = (
        (gx > 0, (gx - 1, gy)),
        (gx < blocks - 1, (gx + 1, gy)),
        (gy > 0, (gx, gy - 1)),
        (gy < groups - 1, (gx, gy + 1)),
    )
    for there, device in sides[:2]:
        @pl.when(there)
        def _(device=device):
            pl.semaphore_signal(barrier, inc=1, device_id=device, device_id_type=MESH)
    for k in range(1, groups):
        pl.semaphore_signal(
            barrier, inc=1, device_id=(gx, lax.rem(gy + k, groups)), device_id_type=MESH
        )

    loads = [
        pltpu.make_async_copy(hist_hbm, hist, load_sem.at[0]),
        pltpu.make_async_copy(v_hbm, V.at[inner], load_sem.at[1]),
        pltpu.make_async_copy(buoy_hbm, buoy, load_sem.at[2]),
        pltpu.make_async_copy(lame_hbm, lame, load_sem.at[3]),
        pltpu.make_async_copy(rig_hbm, rig, load_sem.at[4]),
        pltpu.make_async_copy(mech_hbm, mech_ref, load_sem.at[5]),
        pltpu.make_async_copy(res_hbm, res_ref, load_sem.at[6]),
        pltpu.make_async_copy(own_hbm, own_ref, load_sem.at[7]),
        pltpu.make_async_copy(off_hbm, off_ref, load_sem.at[8]),
    ]
    stress_loads = {
        comp: pltpu.make_async_copy(
            s_hbm.at[comp], S.at[(comp,) + inner[1:]], stress_sem.at[comp]
        )
        for comp in (3, 1, 5, 0, 4, 2)
    }
    for load in list(stress_loads.values()) + loads:
        load.start()

    for ref in (V, S):
        zero_x = jnp.zeros((ref.shape[0], XP, cy, cz), jnp.float32)
        ref[:, pl.ds(0, XP), pl.ds(YP, cy), :] = zero_x
        ref[:, pl.ds(XP + cx, XP), pl.ds(YP, cy), :] = zero_x

        def clear(x, carry, ref=ref):
            zero_y = jnp.zeros((ref.shape[0], YP, cz), jnp.float32)
            ref[:, XP + x, pl.ds(0, YP), :] = zero_y
            ref[:, XP + x, pl.ds(YP + cy, YP), :] = zero_y
            return carry

        lax.fori_loop(0, cx, clear, 0)

    def face_copy(phase, side, faces):
        axis, up = side // 2, side % 2
        send, recv = ((send_x, recv_x), (send_y, recv_y))[axis]
        count = face_slots(faces[axis], bool(up), (cx, cy)[axis])
        return pltpu.make_async_remote_copy(
            src_ref=send.at[phase, up, pl.ds(0, count)],
            dst_ref=recv.at[phase, up, pl.ds(0, count)],
            send_sem=face_send.at[phase, side],
            recv_sem=face_recv.at[phase, side],
            device_id=sides[side][1],
            device_id_type=MESH,
        )

    def row(ref, comp, axis, layer):
        x, y = (XP, YP) if ref is V or ref is S else (0, 0)
        if axis == 0:
            return ref.at[comp, x + layer, pl.ds(y, cy), :]
        return ref.at[comp, pl.ds(x, cx), y + layer, :]

    def coefficient(ref, axis, layer):
        return ref[layer] if axis == 0 else ref[:, layer, :]

    odd = lax.rem(gy, 2) == 1
    even = jnp.logical_not(odd)
    near = ((2, jnp.logical_and(sides[2][0], odd)), (3, jnp.logical_and(sides[3][0], even)))
    far = ((3, jnp.logical_and(sides[3][0], odd)), (2, jnp.logical_and(sides[2][0], even)))
    across = ((0, sides[0][0]), (1, sides[1][0]))

    def send_face(side, phase, ref, faces):
        axis, up = side // 2, side % 2
        send = (send_x, send_y)[axis]
        at = 0
        for comp, layer, wide in face_layers(faces[axis], bool(up), (cx, cy)[axis]):
            value = row(ref, comp, axis, layer)[...]
            head = value.astype(jnp.bfloat16)
            send[phase, up, at] = head
            if wide:
                rest = value - head.astype(jnp.float32)
                send[phase, up, at + 1] = rest.astype(jnp.bfloat16)
            at += 2 if wide else 1
        face_copy(phase, side, faces).start()

    def receive_face(side, phase, faces, apply):
        axis, up = side // 2, side % 2
        recv = (recv_x, recv_y)[axis]
        face_copy(phase, 2 * axis + 1 - up, faces).wait_recv()
        for comp, layer, value in halo_terms(
            faces[axis], not up, (cx, cy)[axis], lambda at: recv[phase, 1 - up, at].astype(jnp.float32)
        ):
            apply(axis, comp, layer, value)

    def at_sides(which, *actions):
        for side, there in which:
            @pl.when(there)
            def _(side=side):
                for action in actions:
                    action(side)

    def exchange(phase, faces, apply, send):
        def receive(side):
            receive_face(side, phase, faces, apply)

        at_sides(across, receive)
        at_sides(near, receive, *send)
        at_sides(far, receive, *send)
        at_sides(across, *send)

    def finish_faces(phase, faces):
        for side in (0, 1, 2, 3):
            @pl.when(sides[side][0])
            def _(side=side):
                face_copy(phase, side, faces).wait_send()

    def add(ref, comp, axis, layer, value):
        place = row(ref, comp, axis, layer)
        place[...] = place[...] + value

    force_of = ({0: 0, 3: 1, 4: 2}, {3: 0, 1: 1, 5: 2})

    def apply_force(axis, comp, layer, value):
        add(V, force_of[axis][comp], axis, layer, coefficient(buoy, axis, layer) * value)

    shear_of = ({1: 3, 2: 4}, {0: 3, 2: 5})

    def apply_strain(target, axis, comp, layer, value):
        mu = coefficient(rig, axis, layer)
        if comp != axis:
            add(target, shear_of[axis][comp], axis, layer, mu * value)
            return
        volume = coefficient(lame, axis, layer) * value
        for normal in range(3):
            extra = volume + 2.0 * mu * value if normal == axis else volume
            add(target, normal, axis, layer, extra)

    level = lax.broadcasted_iota(jnp.int32, (cy, cz), 1)

    def along_z(values, by):
        moved = pltpu.roll(values, (-by) % cz, 1)
        return jnp.where(level < cz - by if by > 0 else level >= -by, moved, 0.0)

    def differ(ref, comp, x, dimension, forward):
        def window(by):
            if dimension == 0:
                return ref[comp, XP + x + by, pl.ds(YP, cy), :]
            if dimension == 1:
                return ref[comp, XP + x, pl.ds(YP + by, cy), :]
            values = ref[comp, XP + x, pl.ds(YP, cy), :]
            return along_z(values, by) if by else values

        if forward:
            return A * (window(1) - window(0)) + B * (window(2) - window(-1))
        return A * (window(0) - window(-1)) + B * (window(1) - window(-2))

    def velocity_inner(x, carry):
        force = (
            differ(S, 0, x, 0, True) + differ(S, 3, x, 1, False) + differ(S, 4, x, 2, False),
            differ(S, 3, x, 0, False) + differ(S, 1, x, 1, True) + differ(S, 5, x, 2, False),
            differ(S, 4, x, 0, False) + differ(S, 5, x, 1, False) + differ(S, 2, x, 2, True),
        )
        factor = buoy[x]
        for comp in range(3):
            place = V.at[comp, XP + x, pl.ds(YP, cy), :]
            place[...] = place[...] + factor * force[comp]
        return carry

    def stress_inner(last, x, carry):
        one = differ(V, 0, x, 0, False)
        two = differ(V, 1, x, 1, False)
        three = differ(V, 2, x, 2, False)
        mu = rig[x]
        volume = lame[x] * (one + two + three)
        rates = (
            volume + 2.0 * mu * one,
            volume + 2.0 * mu * two,
            volume + 2.0 * mu * three,
            mu * (differ(V, 0, x, 1, True) + differ(V, 1, x, 0, True)),
            mu * (differ(V, 0, x, 2, True) + differ(V, 2, x, 0, True)),
            mu * (differ(V, 1, x, 2, True) + differ(V, 2, x, 1, True)),
        )
        for comp in range(6):
            place = S.at[comp, XP + x, pl.ds(YP, cy), :]
            target = s_out.at[comp, x] if last else place
            target[...] = place[...] + rates[comp]
        if last:
            for comp in range(3):
                v_out[comp, x] = V[comp, XP + x, pl.ds(YP, cy), :]
        return carry

    def sweep(body):
        batch = 2 if cx % 2 == 0 else 1

        def several(at, carry):
            for one in range(batch):
                carry = body(batch * at + one, carry)
            return carry

        lax.fori_loop(0, cx // batch, several, 0)

    def source_copy(k):
        return pltpu.make_async_remote_copy(
            src_ref=src,
            dst_ref=gathered.at[:, pl.ds(k * rows, rows)],
            send_sem=src_send.at[k],
            recv_sem=src_recv.at[k],
            device_id=(gx, lax.rem(gy + k, groups)),
            device_id_type=MESH,
        )

    comps = src.shape[0] // (steps + 1)

    def source_terms():
        contract_last = (((1,), (1,)), ((), ()))
        amplitude = lax.dot_general(
            res_ref[...], hist[...], contract_last, preferred_element_type=jnp.float32
        )
        mech = mech_ref[...].astype(jnp.float32)
        spare = jnp.zeros((comps - mech.shape[0], rows), jnp.float32)
        parts = []
        for t in range(steps):
            parts += [mech * amplitude[t : t + 1, :], spare]
        offsets = off_ref[...]
        places = [own_ref[...], offsets // (cy * cz), (offsets // cz) % cy, offsets % cz]
        places = [p.astype(jnp.float32) for p in places]
        parts += [jnp.concatenate(places + [jnp.zeros((comps - 4, rows), jnp.float32)], axis=0)]
        packed = jnp.concatenate(parts, axis=0).astype(jnp.bfloat16)
        src[...] = packed
        gathered[:, pl.ds(0, rows)] = packed

    def source_masks():
        for k in range(groups):
            lanes = pl.ds(k * rows, rows)
            info = gathered[pl.ds(steps * comps, comps), lanes].astype(jnp.float32)
            cell_plane = info[0:1] * float(cx * cy) + info[1:2] * float(cy) + info[2:3]
            plane = lax.broadcasted_iota(jnp.int32, (cx * cy, rows), 0) + gy * (cx * cy)
            plane_hot[:, lanes] = jnp.where(
                plane == cell_plane.astype(jnp.int32), 1.0, 0.0
            ).astype(jnp.bfloat16)
            height = lax.broadcasted_iota(jnp.int32, (cz, rows), 0)
            level_hot[:, lanes] = jnp.where(
                height == info[3:4].astype(jnp.int32), 1.0, 0.0
            ).astype(jnp.bfloat16)

    def insert_sources(t):
        values = gathered[pl.ds(t * comps, comps), :].astype(jnp.float32)
        for comp in range(0, 6, 2):
            spread = jnp.concatenate(
                [
                    level_hot[...] * values[c : c + 1, :].astype(jnp.bfloat16)
                    for c in (comp, comp + 1)
                ],
                axis=0,
            )
            placed = lax.dot_general(
                plane_hot[...], spread, (((1,), (1,)), ((), ())),
                preferred_element_type=jnp.float32,
            )
            for c in range(2):
                place = S.at[comp + c, pl.ds(XP, cx), pl.ds(YP, cy), :]
                place[...] = place[...] + placed[:, c * cz : (c + 1) * cz].reshape(cx, cy, cz)

    arrivals = (
        (gx > 0).astype(jnp.int32) + (gx < blocks - 1).astype(jnp.int32) + (groups - 1)
    )
    pl.semaphore_wait(barrier, arrivals)

    def send_stress(phase):
        return lambda side: send_face(side, phase, S, STRESS_FACES)

    def send_velocity(phase):
        return lambda side: send_face(side, phase, V, VELOCITY_FACES)

    for comp, _ in STRESS_FACES[1]:
        stress_loads.pop(comp).wait()
    at_sides(far, send_stress(0))
    at_sides(near, send_stress(0))
    for load in stress_loads.values():
        load.wait()
    at_sides(across, send_stress(0))
    for load in [loads[0]] + loads[5:]:
        load.wait()
    source_terms()
    for k in range(1, groups):
        source_copy(k).start()
    loads[1].wait()
    loads[2].wait()
    for t in range(steps):
        first, second = 2 * t, 2 * t + 1
        last = t == steps - 1
        sweep(velocity_inner)
        if t > 0:
            insert_sources(t)
        exchange(first, STRESS_FACES, apply_force, (send_velocity(second),))
        if t == 0:
            loads[3].wait()
            loads[4].wait()
        if t == 0 and last:
            for k in range(1, groups):
                source_copy(k).wait_recv()
            source_masks()
            insert_sources(0)
        sweep(functools.partial(stress_inner, last))
        if t == 0 and not last:
            for k in range(1, groups):
                source_copy(k).wait_recv()
            source_masks()
            insert_sources(0)
        exchange(
            second, VELOCITY_FACES,
            functools.partial(apply_strain, s_out if last else S),
            () if last else (send_stress(second + 1),),
        )
    for t in range(steps):
        finish_faces(2 * t, STRESS_FACES)
        finish_faces(2 * t + 1, VELOCITY_FACES)
    for k in range(1, groups):
        source_copy(k).wait_send()


def store_kernel(v_ref, s_ref, v_out, s_out, sem):
    copies = [pltpu.make_async_copy(v_ref, v_out, sem.at[0])]
    half = s_ref.shape[0] // 2
    for part in range(2):
        layers = pl.ds(part * half, half)
        copies.append(pltpu.make_async_copy(s_ref.at[layers], s_out.at[layers], sem.at[1 + part]))
    for copy in copies:
        copy.start()
    for copy in copies:
        copy.wait()


def local(
    velocity, stresses, buoyancy, lame_first, rigidity,
    histories, mechanism, resample, owners, cell_offsets,
):
    groups = lax.axis_size("gy")
    blocks = lax.axis_size("gx")
    rows, samples = histories.shape
    steps = resample.shape[1]
    _, cx, cy, cz = velocity.shape
    comps = 8
    tall = comps * (steps + 1)
    f32, bf16 = jnp.float32, jnp.bfloat16
    hbm = pl.BlockSpec(memory_space=pl.ANY)
    vmem = pl.BlockSpec(memory_space=pltpu.VMEM)
    dma = pltpu.SemaphoreType.DMA
    phases = 2 * steps
    v_last, s_last = pl.pallas_call(
        functools.partial(kernel, groups, blocks, steps),
        out_shape=(
            pltpu.VMEM(velocity.shape, f32),
            pltpu.VMEM(stresses.shape, f32),
        ),
        in_specs=[hbm] * 10,
        out_specs=(vmem, vmem),
        scratch_shapes=[
            pltpu.VMEM((3, cx + 2 * XP, cy + 2 * YP, cz), f32),
            pltpu.VMEM((6, cx + 2 * XP, cy + 2 * YP, cz), f32),
            pltpu.VMEM((cx, cy, cz), f32),
            pltpu.VMEM((cx, cy, cz), f32),
            pltpu.VMEM((cx, cy, cz), f32),
            pltpu.VMEM((rows, samples), bf16),
            pltpu.VMEM((mechanism.shape[1], rows), bf16),
            pltpu.VMEM((steps, samples), bf16),
            pltpu.VMEM((1, rows), jnp.int32),
            pltpu.VMEM((1, rows), jnp.int32),
            pltpu.VMEM((tall, rows), bf16),
            pltpu.VMEM((tall, groups * rows), bf16),
            pltpu.VMEM((cx * cy, groups * rows), bf16),
            pltpu.VMEM((cz, groups * rows), bf16),
            pltpu.VMEM((phases, 2, 9, cy, cz), bf16),
            pltpu.VMEM((phases, 2, 9, cy, cz), bf16),
            pltpu.VMEM((phases, 2, 9, cx, cz), bf16),
            pltpu.VMEM((phases, 2, 9, cx, cz), bf16),
            dma((6,)),
            dma((9,)),
            dma((groups,)),
            dma((groups,)),
            dma((phases, 4)),
            dma((phases, 4)),
        ],
        compiler_params=pltpu.CompilerParams(collective_id=0, has_side_effects=True),
    )(
        velocity, stresses, buoyancy, lame_first, rigidity, histories, mechanism.T, resample.T,
        owners.reshape(1, rows), cell_offsets.reshape(1, rows),
    )
    return pl.pallas_call(
        store_kernel,
        out_shape=(
            jax.ShapeDtypeStruct(velocity.shape, f32),
            jax.ShapeDtypeStruct(stresses.shape, f32),
        ),
        in_specs=[vmem, vmem],
        out_specs=(hbm, hbm),
        scratch_shapes=[dma((3,))],
    )(
        pltpu.with_memory_space_constraint(v_last, pltpu.VMEM),
        pltpu.with_memory_space_constraint(s_last, pltpu.VMEM),
    )


def solution(mesh):
    in_specs = (
        P(None, "gx", "gy", None),
        P(None, "gx", "gy", None),
        P("gx", "gy", None),
        P("gx", "gy", None),
        P("gx", "gy", None),
        P(("gx", "gy"), None),
        P(("gx", "gy"), None),
        P(),
        P(("gx", "gy"), None),
        P(("gx", "gy")),
    )
    out_specs = (P(None, "gx", "gy", None), P(None, "gx", "gy", None))
    return jax.shard_map(local, mesh=mesh, in_specs=in_specs, out_specs=out_specs, check_vma=False)
```

profile of v0, /device:TPU:3, one launch (start us, length us, event | category | flops | bytes accessed | tf_op | source)
XLA Modules:
  0.0 25.4 jit_solution(13726634854708853077)
XLA Ops:
  0.6 23.7 %shard_map.113 = (f32[3,16,16,128]{3,2,1,0:T(8,128)S(1)}, f32[6,16,16,128]{3,2,1,0:T(8,128)S(1)}) custom-call(f32[3,16,16,128]{3,2,1,0:T(8,128)} %v_hbm.1, f32[6,16,16,128]{3,2,1,0:T(8,128)} %s_hbm.1, f32[16,16,128]{2,1,0:T(8,128)} %buoy_hbm.1, f32[16,16,128]{2,1,0:T(8,128)} %lame_hbm.1, f32[16,16,128]{2,1,0:T(8,128)} %rig_hbm.1, bf16[256,512]{1,0:T(8,128)(2,1)} %hist_hbm.1, ...), custom_call_target="tpu_custom_call" | custom-call | tf_op jit(solution)/shard_map/pallas_call | solution.py:424
  24.4 1.0 %shard_map.114 = (f32[3,16,16,128]{3,2,1,0:T(8,128)}, f32[6,16,16,128]{3,2,1,0:T(8,128)}) custom-call(f32[3,16,16,128]{3,2,1,0:T(8,128)S(1)} %get-tuple-element.4.v_ref, f32[6,16,16,128]{3,2,1,0:T(8,128)S(1)} %get-tuple-element.5.s_ref), custom_call_target="tpu_custom_call" | custom-call | tf_op jit(solution)/shard_map/pallas_call | solution.py:463
where the time goes:
time: 25.5 us; the launch traced here: 25.4 us
  Pallas kernels  24.7 us (97%)
  between operations  0.64 us (3%)
    pallas_call x1, Pallas kernels, local(): pl.pallas_call(functools.partial(kernel, groups, blocks, steps), out_shap...  23.7 us
    pallas_call x1, Pallas kernels, local(): pl.pallas_call(store_kernel, out_shape=(jax.ShapeDtypeStruct(velocity.sha...  1.03 us

commit v1 on v0

--- a/solution.py
+++ b/solution.py
@@ -18,37 +18,44 @@
 
 
 def face_layers(faces, up, extent):
+    edge, inward = (extent - 1, -1) if up else (0, 1)
+    out, at = [], 0
+    for comp, forward in faces:
+        wide = forward != up
+        out.append((comp, 0, edge, wide, at))
+        at += 2 if wide else 1
+        if wide:
+            out.append((comp, 1, edge + inward, False, at))
+            at += 1
+    return out
+
+
+def face_slots(faces, up, extent):
+    return sum(2 if wide else 1 for _, _, _, wide, _ in face_layers(faces, up, extent))
+
+
+def unpacker(faces, up, extent, slot):
+    places = {(comp, order): (at, wide) for comp, order, _, wide, at in face_layers(faces, up, extent)}
+
+    def halo(comp, order):
+        at, wide = places[comp, order]
+        value = slot(at).astype(jnp.float32)
+        return value + slot(at + 1).astype(jnp.float32) if wide else value
+
+    return halo
+
+
+def halo_terms(faces, from_low, extent, halo):
+    edge, inward = (0, 1) if from_low else (extent - 1, -1)
+    sign = -1.0 if from_low else 1.0
     out = []
     for comp, forward in faces:
-        if up:
-            out += [(comp, extent - 1, not forward)]
-            out += [] if forward else [(comp, extent - 2, False)]
-        else:
-            out += [(comp, 0, forward)]
-            out += [(comp, 1, False)] if forward else []
-    return out
-
-
-def face_slots(faces, up, extent):
-    return sum(2 if wide else 1 for _, _, wide in face_layers(faces, up, extent))
-
-
-def halo_terms(faces, from_low, extent, halo):
-    out, at = [], 0
-    for comp, forward in faces:
         if from_low == forward:
-            sign = -B if from_low else B
-            out.append((comp, 0 if from_low else extent - 1, sign * halo(at)))
-            at += 1
+            out.append((comp, 0, edge, sign * B * halo(comp, 0)))
             continue
-        first, second = halo(at) + halo(at + 1), halo(at + 2)
-        at += 3
-        if from_low:
-            out.append((comp, 0, -A * first - B * second))
-            out.append((comp, 1, -B * first))
-        else:
-            out.append((comp, extent - 1, A * first + B * second))
-            out.append((comp, extent - 2, B * first))
+        first, second = halo(comp, 0), halo(comp, 1)
+        out.append((comp, 0, edge, sign * A * first + sign * B * second))
+        out.append((comp, 1, edge + inward, sign * B * first))
     return out
 
 
@@ -57,8 +64,9 @@
     v_hbm, s_hbm, buoy_hbm, lame_hbm, rig_hbm, hist_hbm, mech_hbm, res_hbm, own_hbm, off_hbm,
     v_out, s_out,
     V, S, buoy, lame, rig, hist, mech_ref, res_ref, own_ref, off_ref, src, gathered, plane_hot, level_hot,
-    send_x, recv_x, send_y, recv_y,
+    send_x, recv_x, send_y, recv_y, corner_out, corner_in, edge_x, edge_y_out, edge_y, own_x, own_y,
     stress_sem, load_sem, src_send, src_recv, face_send, face_recv,
+    corner_send, corner_recv, edge_send, edge_recv,
 ):
     gx = lax.axis_index("gx")
     gy = lax.axis_index("gy")
@@ -74,6 +82,15 @@
         (gy < groups - 1, (gx, gy + 1)),
     )
     for there, device in sides[:2]:
+        @pl.when(there)
+        def _(device=device):
+            pl.semaphore_signal(barrier, inc=1, device_id=device, device_id_type=MESH)
+    corners = []
+    for ux in range(2):
+        for uy in range(2):
+            there = jnp.logical_and(sides[ux][0], sides[2 + uy][0])
+            corners.append((there, (gx + 2 * ux - 1, gy + 2 * uy - 1)))
+    for there, device in corners:
         @pl.when(there)
         def _(device=device):
             pl.semaphore_signal(barrier, inc=1, device_id=device, device_id_type=MESH)
@@ -146,25 +163,115 @@
     def send_face(side, phase, ref, faces):
         axis, up = side // 2, side % 2
         send = (send_x, send_y)[axis]
-        at = 0
-        for comp, layer, wide in face_layers(faces[axis], bool(up), (cx, cy)[axis]):
+        for comp, _, layer, wide, at in face_layers(faces[axis], bool(up), (cx, cy)[axis]):
             value = row(ref, comp, axis, layer)[...]
             head = value.astype(jnp.bfloat16)
             send[phase, up, at] = head
             if wide:
                 rest = value - head.astype(jnp.float32)
                 send[phase, up, at + 1] = rest.astype(jnp.bfloat16)
-            at += 2 if wide else 1
         face_copy(phase, side, faces).start()
 
-    def receive_face(side, phase, faces, apply):
+    def receive_face(side, phase, faces, apply, partial=None):
         axis, up = side // 2, side % 2
+        extent = (cx, cy)[axis]
         recv = (recv_x, recv_y)[axis]
         face_copy(phase, 2 * axis + 1 - up, faces).wait_recv()
-        for comp, layer, value in halo_terms(
-            faces[axis], not up, (cx, cy)[axis], lambda at: recv[phase, 1 - up, at].astype(jnp.float32)
-        ):
+        arrived = unpacker(faces[axis], not up, extent, lambda at: recv[phase, 1 - up, at])
+        halo = arrived if partial is None else lambda comp, order: arrived(comp, order) + partial(side, comp, order)
+        for comp, _, layer, value in halo_terms(faces[axis], not up, extent, halo):
             apply(axis, comp, layer, value)
+
+    def edge_copy(side):
+        axis, up = side // 2, side % 2
+        if axis == 0:
+            src, dst = buoy.at[pl.ds(cx - 2 if up else 0, 2)], edge_x.at[up]
+        else:
+            src, dst = edge_y_out.at[up], edge_y.at[up]
+        return pltpu.make_async_remote_copy(
+            src_ref=src, dst_ref=dst,
+            send_sem=edge_send.at[side], recv_sem=edge_recv.at[side],
+            device_id=sides[side][1], device_id_type=MESH,
+        )
+
+    def send_edge(side):
+        axis, up = side // 2, side % 2
+        if axis == 1:
+            for order in range(2):
+                edge_y_out[up, order] = buoy[:, cy - 1 - order if up else order, :]
+        edge_copy(side).start()
+
+    def edge_index(axis, up, order):
+        return 1 - order if axis == 0 and up else order
+
+    velocity_places = [
+        [
+            {(comp, order): k for k, (comp, order, *_) in enumerate(face_layers(VELOCITY_FACES[axis], not up, extent))}
+            for up in (False, True)
+        ]
+        for axis, extent in enumerate((cx, cy))
+    ]
+    force_of = ({0: 0, 3: 1, 4: 2}, {3: 0, 1: 1, 5: 2})
+    owns, edges = (own_x, own_y), (edge_x, edge_y)
+
+    def own_part(side, phase):
+        axis, up = side // 2, side % 2
+        send = (send_x, send_y)[axis]
+        halo = unpacker(STRESS_FACES[axis], bool(up), (cx, cy)[axis], lambda at: send[phase, up, at])
+        for comp, order, _, value in halo_terms(STRESS_FACES[axis], bool(up), (cx, cy)[axis], halo):
+            k = velocity_places[axis][up][force_of[axis][comp], order]
+            factor = edges[axis][1 - up, edge_index(axis, 1 - up, order)]
+            owns[axis][up, k] = factor * value
+
+    def partial_velocity(side, comp, order):
+        axis, up = side // 2, side % 2
+        return owns[axis][up, velocity_places[axis][up][comp, order]]
+
+    corner_comps = (0, 1, 3, 4, 5)
+
+    def corner_copy(t, corner):
+        return pltpu.make_async_remote_copy(
+            src_ref=corner_out.at[t, corner], dst_ref=corner_in.at[t, corner],
+            send_sem=corner_send.at[t, corner], recv_sem=corner_recv.at[t, corner],
+            device_id=corners[corner][1], device_id_type=MESH,
+        )
+
+    def send_corner(t, corner):
+        ux, uy = corner // 2, corner % 2
+        for i, comp in enumerate(corner_comps):
+            for xi in range(2):
+                x, y = (cx - 2 if ux else 0) + xi, cy - 2 if uy else 0
+                corner_out[t, corner, pl.ds(4 * i + 2 * xi, 2), :] = S[comp, XP + x, pl.ds(YP + y, 2), :]
+        corner_copy(t, corner).start()
+
+    def receive_corner(t, corner):
+        ups = (corner // 2, corner % 2)
+        corner_copy(t, 3 - corner).wait_recv()
+
+        def stress(comp, orders):
+            xi, yi = (order if up else 1 - order for up, order in zip(ups, orders))
+            return corner_in[t, 3 - corner, pl.ds(4 * corner_comps.index(comp) + 2 * xi + yi, 1), :]
+
+        for axis in range(2):
+            up, other = ups[axis], 1 - axis
+            extent = (cx, cy)[other]
+            for (vcomp, order), k in velocity_places[axis][up].items():
+                edge = edge_index(axis, 1 - up, order)
+
+                def halo(comp, across):
+                    return stress(comp, (order, across) if axis == 0 else (across, order))
+
+                faces = [f for f in STRESS_FACES[other] if force_of[other][f[0]] == vcomp]
+                for _, _, layer, value in halo_terms(faces, not ups[other], extent, halo):
+                    place = owns[axis].at[up, k, pl.ds(layer, 1), :]
+                    place[...] = place[...] + edges[axis][1 - up, edge, pl.ds(layer, 1), :] * value
+
+    def at_corners(*actions):
+        for corner, (there, _) in enumerate(corners):
+            @pl.when(there)
+            def _(corner=corner):
+                for action in actions:
+                    action(corner)
 
     def at_sides(which, *actions):
         for side, there in which:
@@ -173,15 +280,6 @@
                 for action in actions:
                     action(side)
 
-    def exchange(phase, faces, apply, send):
-        def receive(side):
-            receive_face(side, phase, faces, apply)
-
-        at_sides(across, receive)
-        at_sides(near, receive, *send)
-        at_sides(far, receive, *send)
-        at_sides(across, *send)
-
     def finish_faces(phase, faces):
         for side in (0, 1, 2, 3):
             @pl.when(sides[side][0])
@@ -191,8 +289,6 @@
     def add(ref, comp, axis, layer, value):
         place = row(ref, comp, axis, layer)
         place[...] = place[...] + value
-
-    force_of = ({0: 0, 3: 1, 4: 2}, {3: 0, 1: 1, 5: 2})
 
     def apply_force(axis, comp, layer, value):
         add(V, force_of[axis][comp], axis, layer, coefficient(buoy, axis, layer) * value)
@@ -335,60 +431,70 @@
                 place = S.at[comp + c, pl.ds(XP, cx), pl.ds(YP, cy), :]
                 place[...] = place[...] + placed[:, c * cz : (c + 1) * cz].reshape(cx, cy, cz)
 
-    arrivals = (
-        (gx > 0).astype(jnp.int32) + (gx < blocks - 1).astype(jnp.int32) + (groups - 1)
-    )
-    pl.semaphore_wait(barrier, arrivals)
-
-    def send_stress(phase):
-        return lambda side: send_face(side, phase, S, STRESS_FACES)
-
-    def send_velocity(phase):
-        return lambda side: send_face(side, phase, V, VELOCITY_FACES)
-
-    for comp, _ in STRESS_FACES[1]:
-        stress_loads.pop(comp).wait()
-    at_sides(far, send_stress(0))
-    at_sides(near, send_stress(0))
-    for load in stress_loads.values():
-        load.wait()
-    at_sides(across, send_stress(0))
+    arrivals = groups - 1
+    for there, _ in list(sides[:2]) + corners:
+        arrivals += there.astype(jnp.int32)
+
+    def send_stress(t):
+        def send(side):
+            send_face(side, 2 * t, S, STRESS_FACES)
+
+        at_sides(far, send)
+        at_corners(functools.partial(send_corner, t))
+        at_sides(near, send)
+        at_sides(across, send)
+
     for load in [loads[0]] + loads[5:]:
         load.wait()
     source_terms()
+    pl.semaphore_wait(barrier, arrivals)
+    for load in stress_loads.values():
+        load.wait()
+    send_stress(0)
     for k in range(1, groups):
         source_copy(k).start()
     loads[1].wait()
     loads[2].wait()
+    everywhere = far + near + across
+    at_sides(everywhere, send_edge)
     for t in range(steps):
         first, second = 2 * t, 2 * t + 1
         last = t == steps - 1
         sweep(velocity_inner)
+        at_sides(everywhere, lambda side: send_face(side, second, V, VELOCITY_FACES))
         if t > 0:
+            at_sides(everywhere, lambda side: own_part(side, first))
             insert_sources(t)
-        exchange(first, STRESS_FACES, apply_force, (send_velocity(second),))
+        at_sides(across + near + far, lambda side: receive_face(side, first, STRESS_FACES, apply_force))
         if t == 0:
             loads[3].wait()
             loads[4].wait()
-        if t == 0 and last:
-            for k in range(1, groups):
-                source_copy(k).wait_recv()
-            source_masks()
-            insert_sources(0)
+            at_sides(across + near + far, lambda side: edge_copy(2 * (side // 2) + 1 - side % 2).wait_recv())
+            at_sides(everywhere, lambda side: own_part(side, first))
+            if last:
+                for k in range(1, groups):
+                    source_copy(k).wait_recv()
+                source_masks()
+                insert_sources(0)
         sweep(functools.partial(stress_inner, last))
         if t == 0 and not last:
             for k in range(1, groups):
                 source_copy(k).wait_recv()
             source_masks()
             insert_sources(0)
-        exchange(
-            second, VELOCITY_FACES,
-            functools.partial(apply_strain, s_out if last else S),
-            () if last else (send_stress(second + 1),),
-        )
+        at_corners(functools.partial(receive_corner, t))
+        strain = functools.partial(apply_strain, s_out if last else S)
+        at_sides(
+            across + near + far,
+            lambda side: receive_face(side, second, VELOCITY_FACES, strain, partial_velocity),
+        )
+        if not last:
+            send_stress(t + 1)
     for t in range(steps):
         finish_faces(2 * t, STRESS_FACES)
         finish_faces(2 * t + 1, VELOCITY_FACES)
+        at_corners(lambda corner: corner_copy(t, corner).wait_send())
+    at_sides(everywhere, lambda side: edge_copy(side).wait_send())
     for k in range(1, groups):
         source_copy(k).wait_send()
 
@@ -448,12 +554,23 @@
             pltpu.VMEM((phases, 2, 9, cy, cz), bf16),
             pltpu.VMEM((phases, 2, 9, cx, cz), bf16),
             pltpu.VMEM((phases, 2, 9, cx, cz), bf16),
+            pltpu.VMEM((steps, 4, 24, cz), f32),
+            pltpu.VMEM((steps, 4, 24, cz), f32),
+            pltpu.VMEM((2, 2, cy, cz), f32),
+            pltpu.VMEM((2, 2, cx, cz), f32),
+            pltpu.VMEM((2, 2, cx, cz), f32),
+            pltpu.VMEM((2, 5, cy, cz), f32),
+            pltpu.VMEM((2, 5, cx, cz), f32),
             dma((6,)),
             dma((9,)),
             dma((groups,)),
             dma((groups,)),
             dma((phases, 4)),
             dma((phases, 4)),
+            dma((steps, 4)),
+            dma((steps, 4)),
+            dma((4,)),
+            dma((4,)),
         ],
         compiler_params=pltpu.CompilerParams(collective_id=0, has_side_effects=True),
     )(

time: 25.5 us -> 24.8 us (0.973)
  the two profiles are of different devices: /device:TPU:3 before, /device:TPU:0 now
where the time goes in v1:
time: 24.8 us; the launch traced here: 24.7 us
  Pallas kernels  24 us (97%)
  between operations  0.64 us (3%)
    pallas_call x1, Pallas kernels, local(): pl.pallas_call(functools.partial(kernel, groups, blocks, steps), out_shap...  23 us
    pallas_call x1, Pallas kernels, local(): pl.pallas_call(store_kernel, out_shape=(jax.ShapeDtypeStruct(velocity.sha...  1.03 us

profile of v1, /device:TPU:0, one launch (start us, length us, event | category | flops | bytes accessed | tf_op | source)
XLA Modules:
  0.0 24.7 jit_solution(11142495485292429200)
XLA Ops:
  0.6 23.0 %shard_map.113 = (f32[3,16,16,128]{3,2,1,0:T(8,128)S(1)}, f32[6,16,16,128]{3,2,1,0:T(8,128)S(1)}) custom-call(f32[3,16,16,128]{3,2,1,0:T(8,128)} %v_hbm.1, f32[6,16,16,128]{3,2,1,0:T(8,128)} %s_hbm.1, f32[16,16,128]{2,1,0:T(8,128)} %buoy_hbm.1, f32[16,16,128]{2,1,0:T(8,128)} %lame_hbm.1, f32[16,16,128]{2,1,0:T(8,128)} %rig_hbm.1, bf16[256,512]{1,0:T(8,128)(2,1)} %hist_hbm.1, ...), custom_call_target="tpu_custom_call" | custom-call | tf_op jit(solution)/shard_map/pallas_call | solution.py:530
  23.6 1.0 %shard_map.114 = (f32[3,16,16,128]{3,2,1,0:T(8,128)}, f32[6,16,16,128]{3,2,1,0:T(8,128)}) custom-call(f32[3,16,16,128]{3,2,1,0:T(8,128)S(1)} %get-tuple-element.4.v_ref, f32[6,16,16,128]{3,2,1,0:T(8,128)S(1)} %get-tuple-element.5.s_ref), custom_call_target="tpu_custom_call" | custom-call | tf_op jit(solution)/shard_map/pallas_call | solution.py:580

commit v2 on v1

--- a/solution.py
+++ b/solution.py
@@ -64,7 +64,7 @@
     v_hbm, s_hbm, buoy_hbm, lame_hbm, rig_hbm, hist_hbm, mech_hbm, res_hbm, own_hbm, off_hbm,
     v_out, s_out,
     V, S, buoy, lame, rig, hist, mech_ref, res_ref, own_ref, off_ref, src, gathered, plane_hot, level_hot,
-    send_x, recv_x, send_y, recv_y, corner_out, corner_in, edge_x, edge_y_out, edge_y, own_x, own_y,
+    send_x, recv_x, send_y, recv_y, corner_stage, corner_out, corner_in, edge_out_x, edge_in_x, edge_out_y, edge_in_y, edge_x, edge_y, own_x, own_y,
     stress_sem, load_sem, src_send, src_recv, face_send, face_recv,
     corner_send, corner_recv, edge_send, edge_recv,
 ):
@@ -184,25 +184,30 @@
 
     def edge_copy(side):
         axis, up = side // 2, side % 2
-        if axis == 0:
-            src, dst = buoy.at[pl.ds(cx - 2 if up else 0, 2)], edge_x.at[up]
-        else:
-            src, dst = edge_y_out.at[up], edge_y.at[up]
+        out, into = ((edge_out_x, edge_in_x), (edge_out_y, edge_in_y))[axis]
         return pltpu.make_async_remote_copy(
-            src_ref=src, dst_ref=dst,
+            src_ref=out.at[up], dst_ref=into.at[up],
             send_sem=edge_send.at[side], recv_sem=edge_recv.at[side],
             device_id=sides[side][1], device_id_type=MESH,
         )
 
     def send_edge(side):
         axis, up = side // 2, side % 2
-        if axis == 1:
-            for order in range(2):
-                edge_y_out[up, order] = buoy[:, cy - 1 - order if up else order, :]
+        extent, out = (cx, cy)[axis], (edge_out_x, edge_out_y)[axis]
+        near = coefficient(buoy, axis, extent - 1 if up else 0)
+        head = near.astype(jnp.bfloat16)
+        out[up, 0] = head
+        out[up, 1] = (near - head.astype(jnp.float32)).astype(jnp.bfloat16)
+        out[up, 2] = coefficient(buoy, axis, extent - 2 if up else 1).astype(jnp.bfloat16)
         edge_copy(side).start()
 
-    def edge_index(axis, up, order):
-        return 1 - order if axis == 0 and up else order
+    def receive_edge(side):
+        axis, up = side // 2, side % 2
+        into = (edge_in_x, edge_in_y)[axis]
+        edge_copy(2 * axis + 1 - up).wait_recv()
+        arrived = [into[1 - up, k].astype(jnp.float32) for k in range(3)]
+        edges[axis][1 - up, 0] = arrived[0] + arrived[1]
+        edges[axis][1 - up, 1] = arrived[2]
 
     velocity_places = [
         [
@@ -220,14 +225,30 @@
         halo = unpacker(STRESS_FACES[axis], bool(up), (cx, cy)[axis], lambda at: send[phase, up, at])
         for comp, order, _, value in halo_terms(STRESS_FACES[axis], bool(up), (cx, cy)[axis], halo):
             k = velocity_places[axis][up][force_of[axis][comp], order]
-            factor = edges[axis][1 - up, edge_index(axis, 1 - up, order)]
+            factor = edges[axis][1 - up, order]
             owns[axis][up, k] = factor * value
 
     def partial_velocity(side, comp, order):
         axis, up = side // 2, side % 2
         return owns[axis][up, velocity_places[axis][up][comp, order]]
 
-    corner_comps = (0, 1, 3, 4, 5)
+    def corner_terms(ups):
+        out = []
+        for axis in range(2):
+            other = 1 - axis
+            for (vcomp, order), k in velocity_places[axis][ups[axis]].items():
+                faces = [f for f in STRESS_FACES[other] if force_of[other][f[0]] == vcomp]
+                out.append((axis, k, order, faces))
+        return out
+
+    def corner_rows(ups):
+        rows = {}
+        for axis, _, order, faces in corner_terms(ups):
+            def halo(comp, across, axis=axis, order=order):
+                rows.setdefault((comp, order, across) if axis == 0 else (comp, across, order), len(rows))
+                return 0.0
+            halo_terms(faces, not ups[1 - axis], (cx, cy)[1 - axis], halo)
+        return rows
 
     def corner_copy(t, corner):
         return pltpu.make_async_remote_copy(
@@ -238,33 +259,27 @@
 
     def send_corner(t, corner):
         ux, uy = corner // 2, corner % 2
-        for i, comp in enumerate(corner_comps):
-            for xi in range(2):
-                x, y = (cx - 2 if ux else 0) + xi, cy - 2 if uy else 0
-                corner_out[t, corner, pl.ds(4 * i + 2 * xi, 2), :] = S[comp, XP + x, pl.ds(YP + y, 2), :]
+        for (comp, xo, yo), r in corner_rows((1 - ux, 1 - uy)).items():
+            x, y = cx - 1 - xo if ux else xo, cy - 1 - yo if uy else yo
+            corner_stage[corner, pl.ds(r, 1), :] = S[comp, XP + x, pl.ds(YP + y, 1), :]
+        corner_out[t, corner] = corner_stage[corner].astype(jnp.bfloat16)
         corner_copy(t, corner).start()
 
     def receive_corner(t, corner):
         ups = (corner // 2, corner % 2)
         corner_copy(t, 3 - corner).wait_recv()
-
-        def stress(comp, orders):
-            xi, yi = (order if up else 1 - order for up, order in zip(ups, orders))
-            return corner_in[t, 3 - corner, pl.ds(4 * corner_comps.index(comp) + 2 * xi + yi, 1), :]
-
-        for axis in range(2):
-            up, other = ups[axis], 1 - axis
-            extent = (cx, cy)[other]
-            for (vcomp, order), k in velocity_places[axis][up].items():
-                edge = edge_index(axis, 1 - up, order)
-
-                def halo(comp, across):
-                    return stress(comp, (order, across) if axis == 0 else (across, order))
-
-                faces = [f for f in STRESS_FACES[other] if force_of[other][f[0]] == vcomp]
-                for _, _, layer, value in halo_terms(faces, not ups[other], extent, halo):
-                    place = owns[axis].at[up, k, pl.ds(layer, 1), :]
-                    place[...] = place[...] + edges[axis][1 - up, edge, pl.ds(layer, 1), :] * value
+        rows = corner_rows(ups)
+        arrived = corner_in[t, 3 - corner].astype(jnp.float32)
+        for axis, k, order, faces in corner_terms(ups):
+            up = ups[axis]
+
+            def halo(comp, across):
+                r = rows[(comp, order, across) if axis == 0 else (comp, across, order)]
+                return arrived[r : r + 1]
+
+            for _, _, layer, value in halo_terms(faces, not ups[1 - axis], (cx, cy)[1 - axis], halo):
+                place = owns[axis].at[up, k, pl.ds(layer, 1), :]
+                place[...] = place[...] + edges[axis][1 - up, order, pl.ds(layer, 1), :] * value
 
     def at_corners(*actions):
         for corner, (there, _) in enumerate(corners):
@@ -360,7 +375,7 @@
         return carry
 
     def sweep(body):
-        batch = 2 if cx % 2 == 0 else 1
+        batch = max(b for b in (8, 4, 2, 1) if cx % b == 0)
 
         def several(at, carry):
             for one in range(batch):
@@ -440,37 +455,37 @@
             send_face(side, 2 * t, S, STRESS_FACES)
 
         at_sides(far, send)
+        at_sides(near, send)
         at_corners(functools.partial(send_corner, t))
-        at_sides(near, send)
         at_sides(across, send)
 
-    for load in [loads[0]] + loads[5:]:
-        load.wait()
-    source_terms()
+    corner_stage[...] = jnp.zeros_like(corner_stage)
     pl.semaphore_wait(barrier, arrivals)
     for load in stress_loads.values():
         load.wait()
     send_stress(0)
+    for load in [loads[0]] + loads[5:]:
+        load.wait()
+    source_terms()
     for k in range(1, groups):
         source_copy(k).start()
     loads[1].wait()
     loads[2].wait()
     everywhere = far + near + across
-    at_sides(everywhere, send_edge)
     for t in range(steps):
         first, second = 2 * t, 2 * t + 1
         last = t == steps - 1
         sweep(velocity_inner)
         at_sides(everywhere, lambda side: send_face(side, second, V, VELOCITY_FACES))
-        if t > 0:
+        if t == 0:
+            at_sides(everywhere, send_edge)
+        else:
             at_sides(everywhere, lambda side: own_part(side, first))
             insert_sources(t)
         at_sides(across + near + far, lambda side: receive_face(side, first, STRESS_FACES, apply_force))
         if t == 0:
             loads[3].wait()
             loads[4].wait()
-            at_sides(across + near + far, lambda side: edge_copy(2 * (side // 2) + 1 - side % 2).wait_recv())
-            at_sides(everywhere, lambda side: own_part(side, first))
             if last:
                 for k in range(1, groups):
                     source_copy(k).wait_recv()
@@ -482,6 +497,8 @@
                 source_copy(k).wait_recv()
             source_masks()
             insert_sources(0)
+        if t == 0:
+            at_sides(across + near + far, receive_edge, lambda side: own_part(side, first))
         at_corners(functools.partial(receive_corner, t))
         strain = functools.partial(apply_strain, s_out if last else S)
         at_sides(
@@ -554,10 +571,14 @@
             pltpu.VMEM((phases, 2, 9, cy, cz), bf16),
             pltpu.VMEM((phases, 2, 9, cx, cz), bf16),
             pltpu.VMEM((phases, 2, 9, cx, cz), bf16),
-            pltpu.VMEM((steps, 4, 24, cz), f32),
-            pltpu.VMEM((steps, 4, 24, cz), f32),
+            pltpu.VMEM((4, 16, cz), f32),
+            pltpu.VMEM((steps, 4, 16, cz), bf16),
+            pltpu.VMEM((steps, 4, 16, cz), bf16),
+            pltpu.VMEM((2, 3, cy, cz), bf16),
+            pltpu.VMEM((2, 3, cy, cz), bf16),
+            pltpu.VMEM((2, 3, cx, cz), bf16),
+            pltpu.VMEM((2, 3, cx, cz), bf16),
             pltpu.VMEM((2, 2, cy, cz), f32),
-            pltpu.VMEM((2, 2, cx, cz), f32),
             pltpu.VMEM((2, 2, cx, cz), f32),
             pltpu.VMEM((2, 5, cy, cz), f32),
             pltpu.VMEM((2, 5, cx, cz), f32),

time: 24.8 us -> 21.7 us (0.88)
  Pallas kernels: 24 us -> 20.9 us
    pallas_call x1, Pallas kernels: 23 us -> 19.9 us  [local(): pl.pallas_call(functools.partial(kernel, groups, blocks, steps), out_shap...]
where the time goes in v2:
time: 21.7 us; the launch traced here: 21.6 us
  Pallas kernels  20.9 us (96%)
  between operations  0.64 us (3%)
    pallas_call x1, Pallas kernels, local(): pl.pallas_call(functools.partial(kernel, groups, blocks, steps), out_shap...  19.9 us
    pallas_call x1, Pallas kernels, local(): pl.pallas_call(store_kernel, out_shape=(jax.ShapeDtypeStruct(velocity.sha...  1.03 us

profile of v2, /device:TPU:0, one launch (start us, length us, event | category | flops | bytes accessed | tf_op | source)
XLA Modules:
  0.0 21.6 jit_solution(3252097965437214051)
XLA Ops:
  0.6 19.9 %shard_map.113 = (f32[3,16,16,128]{3,2,1,0:T(8,128)S(1)}, f32[6,16,16,128]{3,2,1,0:T(8,128)S(1)}) custom-call(f32[3,16,16,128]{3,2,1,0:T(8,128)} %v_hbm.1, f32[6,16,16,128]{3,2,1,0:T(8,128)} %s_hbm.1, f32[16,16,128]{2,1,0:T(8,128)} %buoy_hbm.1, f32[16,16,128]{2,1,0:T(8,128)} %lame_hbm.1, f32[16,16,128]{2,1,0:T(8,128)} %rig_hbm.1, bf16[256,512]{1,0:T(8,128)(2,1)} %hist_hbm.1, ...), custom_call_target="tpu_custom_call" | custom-call | tf_op jit(solution)/shard_map/pallas_call | solution.py:547
  20.5 1.0 %shard_map.114 = (f32[3,16,16,128]{3,2,1,0:T(8,128)}, f32[6,16,16,128]{3,2,1,0:T(8,128)}) custom-call(f32[3,16,16,128]{3,2,1,0:T(8,128)S(1)} %get-tuple-element.4.v_ref, f32[6,16,16,128]{3,2,1,0:T(8,128)S(1)} %get-tuple-element.5.s_ref), custom_call_target="tpu_custom_call" | custom-call | tf_op jit(solution)/shard_map/pallas_call | solution.py:601

commit v3 on v2

--- a/solution.py
+++ b/solution.py
@@ -12,6 +12,8 @@
 MESH = pl.DeviceIdType.MESH
 XP = 2
 YP = 8
+CAP = 64
+BUOYANCY = (0.45, 0.15 / 32767.0)
 
 STRESS_FACES = (((0, True), (3, False), (4, False)), ((3, False), (1, True), (5, False)))
 VELOCITY_FACES = (((0, False), (1, True), (2, True)), ((0, True), (1, False), (2, True)))
@@ -63,7 +65,7 @@
     groups, blocks, steps,
     v_hbm, s_hbm, buoy_hbm, lame_hbm, rig_hbm, hist_hbm, mech_hbm, res_hbm, own_hbm, off_hbm,
     v_out, s_out,
-    V, S, buoy, lame, rig, hist, mech_ref, res_ref, own_ref, off_ref, src, gathered, plane_hot, level_hot,
+    V, S, buoy, lame, rig, hist, mech_ref, res_ref, own_ref, off_ref, select, src, gathered, values, plane_hot, level_hot,
     send_x, recv_x, send_y, recv_y, corner_stage, corner_out, corner_in, edge_out_x, edge_in_x, edge_out_y, edge_in_y, edge_x, edge_y, own_x, own_y,
     stress_sem, load_sem, src_send, src_recv, face_send, face_recv,
     corner_send, corner_recv, edge_send, edge_recv,
@@ -116,7 +118,7 @@
         )
         for comp in (3, 1, 5, 0, 4, 2)
     }
-    for load in list(stress_loads.values()) + loads:
+    for load in [loads[7]] + list(stress_loads.values()) + loads[:7] + loads[8:]:
         load.start()
 
     for ref in (V, S):
@@ -149,7 +151,9 @@
         x, y = (XP, YP) if ref is V or ref is S else (0, 0)
         if axis == 0:
             return ref.at[comp, x + layer, pl.ds(y, cy), :]
-        return ref.at[comp, pl.ds(x, cx), y + layer, :]
+        _, planes, height, _ = ref.shape
+        flat = ref.reshape(ref.shape[0], planes * height, cz)
+        return flat.at[comp, pl.ds(x * height + y + layer, cx, stride=height), :]
 
     def coefficient(ref, axis, layer):
         return ref[layer] if axis == 0 else ref[:, layer, :]
@@ -194,20 +198,20 @@
     def send_edge(side):
         axis, up = side // 2, side % 2
         extent, out = (cx, cy)[axis], (edge_out_x, edge_out_y)[axis]
-        near = coefficient(buoy, axis, extent - 1 if up else 0)
-        head = near.astype(jnp.bfloat16)
-        out[up, 0] = head
-        out[up, 1] = (near - head.astype(jnp.float32)).astype(jnp.bfloat16)
-        out[up, 2] = coefficient(buoy, axis, extent - 2 if up else 1).astype(jnp.bfloat16)
+        middle, grain = BUOYANCY
+        for order in range(2):
+            value = coefficient(buoy, axis, extent - 1 - order if up else order)
+            coded = jnp.clip(jnp.round((value - middle) * (1.0 / grain)), -32767.0, 32767.0)
+            out[up, order] = coded.astype(jnp.int32).astype(jnp.int16)
         edge_copy(side).start()
 
     def receive_edge(side):
         axis, up = side // 2, side % 2
         into = (edge_in_x, edge_in_y)[axis]
         edge_copy(2 * axis + 1 - up).wait_recv()
-        arrived = [into[1 - up, k].astype(jnp.float32) for k in range(3)]
-        edges[axis][1 - up, 0] = arrived[0] + arrived[1]
-        edges[axis][1 - up, 1] = arrived[2]
+        middle, grain = BUOYANCY
+        for order in range(2):
+            edges[axis][1 - up, order] = into[1 - up, order].astype(jnp.int32).astype(jnp.float32) * grain + middle
 
     velocity_places = [
         [
@@ -385,62 +389,87 @@
         lax.fori_loop(0, cx // batch, several, 0)
 
     def source_copy(k):
+        owner = lax.rem(gy + k, groups)
         return pltpu.make_async_remote_copy(
-            src_ref=src,
-            dst_ref=gathered.at[:, pl.ds(k * rows, rows)],
+            src_ref=src.at[owner],
+            dst_ref=gathered.at[k],
             send_sem=src_send.at[k],
             recv_sem=src_recv.at[k],
-            device_id=(gx, lax.rem(gy + k, groups)),
+            device_id=(gx, owner),
             device_id_type=MESH,
         )
 
-    comps = src.shape[0] // (steps + 1)
+    comps = 8
+    tall = src.shape[1]
+    contract_last = (((1,), (1,)), ((), ()))
+
+    def source_slots():
+        own = own_ref[...]
+        padded = -(-groups // 16) * 16
+        mine = (lax.broadcasted_iota(jnp.int32, (padded, rows), 0) == own).astype(jnp.float32)
+        before = lax.broadcasted_iota(jnp.int32, (rows, rows), 0) <= lax.broadcasted_iota(jnp.int32, (rows, rows), 1)
+        counts = jnp.dot(
+            mine.astype(jnp.bfloat16), before.astype(jnp.float32).astype(jnp.bfloat16),
+            preferred_element_type=jnp.float32,
+        )
+        rank = jnp.sum(mine * counts, axis=0, keepdims=True).astype(jnp.int32)
+        slot = own * (2 * CAP) + rank - 1
+        for owner in range(groups):
+            lane = lax.broadcasted_iota(jnp.int32, (2 * CAP, rows), 0) + owner * 2 * CAP
+            for part in range(2):
+                select[pl.ds(owner * 2 * CAP, 2 * CAP), pl.ds(part * rows, rows)] = (
+                    (lane == slot + part * CAP).astype(jnp.float32).astype(jnp.bfloat16)
+                )
 
     def source_terms():
-        contract_last = (((1,), (1,)), ((), ()))
         amplitude = lax.dot_general(
             res_ref[...], hist[...], contract_last, preferred_element_type=jnp.float32
         )
         mech = mech_ref[...].astype(jnp.float32)
         spare = jnp.zeros((comps - mech.shape[0], rows), jnp.float32)
-        parts = []
+        offsets = off_ref[...]
+        places = [offsets // (cy * cz), (offsets // cz) % cy, offsets % cz]
+        places = [p.astype(jnp.float32) for p in places]
+        parts = places + [jnp.zeros((comps - 3, rows), jnp.float32)]
         for t in range(steps):
             parts += [mech * amplitude[t : t + 1, :], spare]
-        offsets = off_ref[...]
-        places = [own_ref[...], offsets // (cy * cz), (offsets // cz) % cy, offsets % cz]
-        places = [p.astype(jnp.float32) for p in places]
-        parts += [jnp.concatenate(places + [jnp.zeros((comps - 4, rows), jnp.float32)], axis=0)]
-        packed = jnp.concatenate(parts, axis=0).astype(jnp.bfloat16)
-        src[...] = packed
-        gathered[:, pl.ds(0, rows)] = packed
+        parts += [jnp.zeros((2 * tall - comps * (steps + 1), rows), jnp.float32)] if 2 * tall > comps * (steps + 1) else []
+        packed = jnp.concatenate(parts, axis=0)
+        packed = jnp.concatenate([packed[:tall], packed[tall:]], axis=1).astype(jnp.bfloat16)
+        chosen = lax.dot_general(
+            packed, select[...], contract_last, preferred_element_type=jnp.float32
+        ).astype(jnp.bfloat16)
+        for owner in range(groups):
+            src[owner] = chosen[:, owner * 2 * CAP : (owner + 1) * 2 * CAP]
+        gathered[0] = src[gy]
 
     def source_masks():
-        for k in range(groups):
-            lanes = pl.ds(k * rows, rows)
-            info = gathered[pl.ds(steps * comps, comps), lanes].astype(jnp.float32)
-            cell_plane = info[0:1] * float(cx * cy) + info[1:2] * float(cy) + info[2:3]
-            plane = lax.broadcasted_iota(jnp.int32, (cx * cy, rows), 0) + gy * (cx * cy)
-            plane_hot[:, lanes] = jnp.where(
-                plane == cell_plane.astype(jnp.int32), 1.0, 0.0
-            ).astype(jnp.bfloat16)
-            height = lax.broadcasted_iota(jnp.int32, (cz, rows), 0)
-            level_hot[:, lanes] = jnp.where(
-                height == info[3:4].astype(jnp.int32), 1.0, 0.0
-            ).astype(jnp.bfloat16)
+        first_half = lax.broadcasted_iota(jnp.int32, (tall, 2 * CAP), 1) < CAP
+        for pair in range(groups // 2):
+            low, high = (gathered[2 * pair + i].astype(jnp.float32) for i in range(2))
+            lanes = pl.ds(pair * 2 * CAP, 2 * CAP)
+            values[pl.ds(0, tall), lanes] = jnp.where(first_half, low, pltpu.roll(high, CAP, 1))
+            values[pl.ds(tall, tall), lanes] = jnp.where(first_half, pltpu.roll(low, CAP, 1), high)
+        info = values[pl.ds(0, comps), :]
+        count = info.shape[1]
+        cell_plane = info[0:1] * float(cy) + info[1:2]
+        plane = lax.broadcasted_iota(jnp.int32, (cx * cy, count), 0)
+        plane_hot[...] = jnp.where(plane == cell_plane.astype(jnp.int32), 1.0, 0.0).astype(jnp.bfloat16)
+        height = lax.broadcasted_iota(jnp.int32, (cz, count), 0)
+        level_hot[...] = jnp.where(height == info[2:3].astype(jnp.int32), 1.0, 0.0).astype(jnp.bfloat16)
 
     def insert_sources(t):
-        values = gathered[pl.ds(t * comps, comps), :].astype(jnp.float32)
+        terms = values[pl.ds((t + 1) * comps, comps), :]
         for comp in range(0, 6, 2):
             spread = jnp.concatenate(
                 [
-                    level_hot[...] * values[c : c + 1, :].astype(jnp.bfloat16)
+                    level_hot[...] * terms[c : c + 1, :].astype(jnp.bfloat16)
                     for c in (comp, comp + 1)
                 ],
                 axis=0,
             )
             placed = lax.dot_general(
-                plane_hot[...], spread, (((1,), (1,)), ((), ())),
-                preferred_element_type=jnp.float32,
+                plane_hot[...], spread, contract_last, preferred_element_type=jnp.float32
             )
             for c in range(2):
                 place = S.at[comp + c, pl.ds(XP, cx), pl.ds(YP, cy), :]
@@ -464,8 +493,10 @@
     for load in stress_loads.values():
         load.wait()
     send_stress(0)
-    for load in [loads[0]] + loads[5:]:
+    for load in [loads[0], loads[5], loads[6], loads[8]]:
         load.wait()
+    loads[7].wait()
+    source_slots()
     source_terms()
     for k in range(1, groups):
         source_copy(k).start()
@@ -537,8 +568,7 @@
     rows, samples = histories.shape
     steps = resample.shape[1]
     _, cx, cy, cz = velocity.shape
-    comps = 8
-    tall = comps * (steps + 1)
+    tall = 8 * -(-(steps + 1) // 2)
     f32, bf16 = jnp.float32, jnp.bfloat16
     hbm = pl.BlockSpec(memory_space=pl.ANY)
     vmem = pl.BlockSpec(memory_space=pltpu.VMEM)
@@ -563,10 +593,12 @@
             pltpu.VMEM((steps, samples), bf16),
             pltpu.VMEM((1, rows), jnp.int32),
             pltpu.VMEM((1, rows), jnp.int32),
-            pltpu.VMEM((tall, rows), bf16),
-            pltpu.VMEM((tall, groups * rows), bf16),
-            pltpu.VMEM((cx * cy, groups * rows), bf16),
-            pltpu.VMEM((cz, groups * rows), bf16),
+            pltpu.VMEM((groups * 2 * CAP, 2 * rows), bf16),
+            pltpu.VMEM((groups, tall, 2 * CAP), bf16),
+            pltpu.VMEM((groups, tall, 2 * CAP), bf16),
+            pltpu.VMEM((2 * tall, groups * CAP), f32),
+            pltpu.VMEM((cx * cy, groups * CAP), bf16),
+            pltpu.VMEM((cz, groups * CAP), bf16),
             pltpu.VMEM((phases, 2, 9, cy, cz), bf16),
             pltpu.VMEM((phases, 2, 9, cy, cz), bf16),
             pltpu.VMEM((phases, 2, 9, cx, cz), bf16),
@@ -574,10 +606,10 @@
             pltpu.VMEM((4, 16, cz), f32),
             pltpu.VMEM((steps, 4, 16, cz), bf16),
             pltpu.VMEM((steps, 4, 16, cz), bf16),
-            pltpu.VMEM((2, 3, cy, cz), bf16),
-            pltpu.VMEM((2, 3, cy, cz), bf16),
-            pltpu.VMEM((2, 3, cx, cz), bf16),
-            pltpu.VMEM((2, 3, cx, cz), bf16),
+            pltpu.VMEM((2, 2, cy, cz), jnp.int16),
+            pltpu.VMEM((2, 2, cy, cz), jnp.int16),
+            pltpu.VMEM((2, 2, cx, cz), jnp.int16),
+            pltpu.VMEM((2, 2, cx, cz), jnp.int16),
             pltpu.VMEM((2, 2, cy, cz), f32),
             pltpu.VMEM((2, 2, cx, cz), f32),
             pltpu.VMEM((2, 5, cy, cz), f32),

time: 21.7 us -> 20.7 us (0.954)
  Pallas kernels: 20.9 us -> 19.9 us
    pallas_call x1, Pallas kernels: 19.9 us -> 18.8 us  [local(): pl.pallas_call(functools.partial(kernel, groups, blocks, steps), out_shap...]
where the time goes in v3:
time: 20.7 us; the launch traced here: 20.5 us
  Pallas kernels  19.9 us (96%)
  between operations  0.64 us (3%)
    pallas_call x1, Pallas kernels, local(): pl.pallas_call(functools.partial(kernel, groups, blocks, steps), out_shap...  18.8 us
    pallas_call x1, Pallas kernels, local(): pl.pallas_call(store_kernel, out_shape=(jax.ShapeDtypeStruct(velocity.sha...  1.03 us

profile of v3, /device:TPU:0, one launch (start us, length us, event | category | flops | bytes accessed | tf_op | source)
XLA Modules:
  0.0 20.5 jit_solution(6008474289659199968)
XLA Ops:
  0.6 18.8 %shard_map.113 = (f32[3,16,16,128]{3,2,1,0:T(8,128)S(1)}, f32[6,16,16,128]{3,2,1,0:T(8,128)S(1)}) custom-call(f32[3,16,16,128]{3,2,1,0:T(8,128)} %v_hbm.1, f32[6,16,16,128]{3,2,1,0:T(8,128)} %s_hbm.1, f32[16,16,128]{2,1,0:T(8,128)} %buoy_hbm.1, f32[16,16,128]{2,1,0:T(8,128)} %lame_hbm.1, f32[16,16,128]{2,1,0:T(8,128)} %rig_hbm.1, bf16[256,512]{1,0:T(8,128)(2,1)} %hist_hbm.1, ...), custom_call_target="tpu_custom_call" | custom-call | tf_op jit(solution)/shard_map/pallas_call | solution.py:577
  19.5 1.0 %shard_map.114 = (f32[3,16,16,128]{3,2,1,0:T(8,128)}, f32[6,16,16,128]{3,2,1,0:T(8,128)}) custom-call(f32[3,16,16,128]{3,2,1,0:T(8,128)S(1)} %get-tuple-element.4.v_ref, f32[6,16,16,128]{3,2,1,0:T(8,128)S(1)} %get-tuple-element.5.s_ref), custom_call_target="tpu_custom_call" | custom-call | tf_op jit(solution)/shard_map/pallas_call | solution.py:633
